TPU v7x, 32 devices: a whole 2x2x4 slice. The times are simulated.
32 devices in a mesh: dp: 4 (over y, x), tensor: 8 (over z, core).
Axes of the slice: x: 2, y: 2, z: 4, core: 2. Of those that a mesh axis runs over, the one named last changes fastest.
Arguments:
- tokens: bfloat16 [2048, 4096], P(('dp', 'tensor')), parts along dimension 0, may hold values from -6 to 6
- norm_gain: float32 [4096], replicated, may hold values from 0.5 to 1.5
- gate_weight: bfloat16 [4096, 14336], P(None, 'tensor'), may hold values from -0.09375 to 0.09375
- up_weight: bfloat16 [4096, 14336], P(None, 'tensor'), may hold values from -0.09375 to 0.09375
- down_weight: bfloat16 [14336, 4096], P('tensor'), may hold values from -0.0625 to 0.0625
Outputs:
- mixed: bfloat16 [2048, 4096], P('dp', 'tensor'), parts along dimension 0
There are 4 independent parts, one for each index of `dp`. A program takes and returns all parts, laid end to end along the dimension named above; an argument that names none is the same for every part. Nothing has to cross between parts.
All inputs are finite; a program needn't handle non-finite values.
Results may differ from a plain program's by a relative error of at most 0.0053.
Values may be sent and summed in bfloat16 or wider, within the bound.
A program may use at most 128 MiB of HBM per device.

v0:
```python
import functools

import jax
import jax.numpy as jnp
from jax import lax
from jax.experimental import pallas as pl
from jax.experimental.pallas import tpu as pltpu
from jax.sharding import PartitionSpec as P

HALVES = 2
VMEM_LIMIT = 67043328


def block_kernel(
    n, tok, gain, gw, uw, dw, out,
    gwv, uwv, dwv, every, normed, hidden, part, peer, arrived, acc,
    load_sem, own_sem, ag_recv, ag_send, peer_send, peer_recv, rs_send, rs_recv,
):
    H = HALVES
    dp = lax.axis_index("dp")
    me = lax.axis_index("tensor")
    C = n // 2
    p, c = me // 2, me % 2
    rows, D = tok.shape
    r = rows // H
    T = n * r
    F = gwv.shape[1]
    width = D // n
    partner = (dp, 2 * p + (1 - c))
    right = (dp, lax.rem(me + 2, n))
    left = (dp, lax.rem(me + n - 2, n))
    has_right, has_left = p < C - 1, p > 0

    loads = [pltpu.make_async_copy(a, b, load_sem.at[k]) for k, (a, b) in enumerate(((gw, gwv), (uw, uwv), (dw, dwv)))]

    def block(h, t):
        return every.at[h, pl.ds(pl.multiple_of(t * r, r), r), :]

    own = [pltpu.make_async_copy(tok.at[pl.ds(h * r, r), :], block(h, me), own_sem.at[h]) for h in range(H)]
    for copy in own:
        copy.start()
    for copy in loads:
        copy.start()

    barrier = pltpu.get_barrier_semaphore()

    def greet(device):
        pl.semaphore_signal(barrier, inc=1, device_id=device, device_id_type=pl.DeviceIdType.MESH)

    greet(partner)
    pl.when(has_right)(lambda: greet(right))
    pl.when(has_left)(lambda: greet(left))
    pl.semaphore_wait(barrier, 1 + has_right.astype(jnp.int32) + has_left.astype(jnp.int32))

    def remote(src, dst, s, d, device):
        return pltpu.make_async_remote_copy(
            src_ref=src, dst_ref=dst, send_sem=s, recv_sem=d, device_id=device, device_id_type=pl.DeviceIdType.MESH
        )

    def gather(h, t, way):
        return remote(block(h, t), block(h, t), ag_send.at[way, h, t], ag_recv.at[h, t], (right, left, partner)[way])

    def gather_first(h):
        own[h].wait()
        pl.when(has_right)(lambda: gather(h, me, 0).start())
        pl.when(has_left)(lambda: gather(h, me, 1).start())
        gather(h, me, 2).start()

    def gather_step(h, s):
        @pl.when(p - s >= 0)
        def _():
            t = me - 2 * s
            gather(h, t, 2).wait_recv()
            pl.when(has_right)(lambda: gather(h, t, 0).start())
            gather(h, t, 2).start()

        @pl.when(p + s <= C - 1)
        def _():
            t = me + 2 * s
            gather(h, t, 2).wait_recv()
            pl.when(has_left)(lambda: gather(h, t, 1).start())
            gather(h, t, 2).start()

    def gather_last(h):
        for q in range(C):
            gather(h, 2 * q + (1 - c), 2).wait_recv()

    def gather_drain(h):
        for q in range(C):
            t = 2 * q + c
            pl.when((q <= p) & has_right)(lambda: gather(h, t, 0).wait_send())
            pl.when((q >= p) & has_left)(lambda: gather(h, t, 1).wait_send())
            gather(h, t, 2).wait_send()

    def to_peer(h, q):
        return remote(part.at[h, 2 * q + (1 - c)], peer.at[h, q], peer_send.at[h, q], peer_recv.at[h, q], partner)

    def to_right(h, q):
        return remote(part.at[h, 2 * q + c], arrived.at[h, q], rs_send.at[h, q], rs_recv.at[h, q], right)

    def to_left(h, q):
        slot = jnp.where(q == p - 1, C, q)
        return remote(part.at[h, 2 * q + c], arrived.at[h, slot], rs_send.at[h, q], rs_recv.at[h, slot], left)

    def landed(h, slot):
        remote(arrived.at[h, slot], arrived.at[h, slot], rs_send.at[h, 0], rs_recv.at[h, slot], partner).wait_recv()

    def scatter_first(h):
        for q in range(C):
            to_peer(h, q).wait_recv()
            t = 2 * q + c
            part[h, t] = (part[h, t].astype(jnp.float32) + peer[h, q].astype(jnp.float32)).astype(jnp.bfloat16)

        @pl.when(p == 0)
        def _():
            for q in reversed(range(1, C)):
                to_right(h, q).start()

        @pl.when(p == C - 1)
        def _():
            for q in range(C - 1):
                to_left(h, q).start()

    def add_arrived(h, q):
        landed(h, q)
        t = 2 * q + c
        part[h, t] = (part[h, t].astype(jnp.float32) + arrived[h, q].astype(jnp.float32)).astype(jnp.bfloat16)

    def scatter_step(h, j):
        def rightward():
            q = C - 1 - j

            @pl.when((q > p) & has_left)
            def _():
                add_arrived(h, q)
                to_right(h, q).start()

        def leftward():
            @pl.when((j < p) & has_right)
            def _():
                add_arrived(h, j)
                to_left(h, j).start()

        @pl.when(2 * p < C)
        def _():
            rightward()
            leftward()

        @pl.when(2 * p >= C)
        def _():
            leftward()
            rightward()

    def scatter_last(h):
        lanes = pl.ds(pl.multiple_of(me * width, width), width)
        acc[...] = every[h, :, lanes].astype(jnp.float32) + part[h, me].astype(jnp.float32)

        @pl.when(has_left)
        def _():
            landed(h, p)
            acc[...] += arrived[h, p].astype(jnp.float32)

        @pl.when(has_right)
        def _():
            landed(h, C)
            acc[...] += arrived[h, C].astype(jnp.float32)

        for t in range(n):
            out[t * rows + h * r : t * rows + (h + 1) * r, :] = acc[t * r : (t + 1) * r, :].astype(jnp.bfloat16)

    def scatter_drain(h):
        for q in range(C):
            to_peer(h, q).wait_send()
            pl.when(q > p)(lambda: to_right(h, q).wait_send())
            pl.when(q < p)(lambda: to_left(h, q).wait_send())

    def norm(h):
        step = 16

        @pl.loop(0, T // step)
        def _(i):
            at = pl.ds(pl.multiple_of(i * step, step), step)
            wide = every[h, at, :].astype(jnp.float32)
            square_mean = jnp.mean(wide * wide, axis=1, keepdims=True)
            normed[at, :] = (wide * gain[...] / jnp.sqrt(square_mean + 1e-05)).astype(jnp.bfloat16)

    def expand(hooks):
        tile = 256 if F % 256 == 0 else 128

        @pl.loop(0, F // tile)
        def _(i):
            for k, hook in hooks:
                pl.when(i == min(k, F // tile - 1))(hook)
            at = pl.ds(pl.multiple_of(i * tile, tile), tile)
            gate = jnp.dot(normed[...], gwv[:, at], preferred_element_type=jnp.float32)
            up = jnp.dot(normed[...], uwv[:, at], preferred_element_type=jnp.float32)
            hidden[:, at] = (jax.nn.silu(gate) * up).astype(jnp.bfloat16)

    def reduce(h, hooks):
        @pl.loop(0, n)
        def _(i):
            for k, hook in hooks:
                pl.when(i == min(k, n - 1))(hook)
            q = lax.rem(i, C)
            t = 2 * q + jnp.where(i < C, 1 - c, c)
            at = pl.ds(pl.multiple_of(t * width, width), width)
            part[h, t] = jnp.dot(hidden[...], dwv[:, at], preferred_element_type=jnp.float32).astype(jnp.bfloat16)
            pl.when(i < C)(lambda: to_peer(h, q).start())

    gather_first(0)
    for s in range(1, C):
        gather_step(0, s)
    gather_first(1)
    gather_last(0)
    norm(0)
    loads[0].wait()
    loads[1].wait()
    expand([(4, lambda: gather_step(1, 1))])
    loads[2].wait()
    reduce(0, [(2, lambda: gather_step(1, 2)) if C > 2 else (2, lambda: None)])
    scatter_first(0)
    for s in range(3, C):
        gather_step(1, s)
    gather_last(1)
    norm(1)
    expand([(3, lambda: scatter_step(0, 0))])
    reduce(1, [(2, lambda: scatter_step(0, 1))])
    scatter_first(1)
    for j in range(2, C):
        scatter_step(0, j)
    for j in range(C):
        scatter_step(1, j)
    scatter_last(0)
    scatter_last(1)
    for h in range(H):
        gather_drain(h)
        scatter_drain(h)


def on_device(n, tokens, norm_gain, gate_weight, up_weight, down_weight):
    H = HALVES
    rows, D = tokens.shape
    F = gate_weight.shape[1]
    C = n // 2
    T, width = n * rows // H, D // n
    bf16 = jnp.bfloat16
    any_space, vmem = pl.BlockSpec(memory_space=pl.ANY), pl.BlockSpec(memory_space=pltpu.VMEM)
    dma = pltpu.SemaphoreType.DMA
    return pl.pallas_call(
        functools.partial(block_kernel, n),
        out_shape=jax.ShapeDtypeStruct((n * rows, width), bf16),
        in_specs=[any_space, vmem, any_space, any_space, any_space],
        out_specs=vmem,
        scratch_shapes=[
            pltpu.VMEM((D, F), bf16),
            pltpu.VMEM((D, F), bf16),
            pltpu.VMEM((F, D), bf16),
            pltpu.VMEM((H, T, D), bf16),
            pltpu.VMEM((T, D), bf16),
            pltpu.VMEM((T, F), bf16),
            pltpu.VMEM((H, n, T, width), bf16),
            pltpu.VMEM((H, C, T, width), bf16),
            pltpu.VMEM((H, C + 1, T, width), bf16),
            pltpu.VMEM((T, width), jnp.float32),
            dma((3,)),
            dma((H,)),
            dma((H, n)),
            dma((3, H, n)),
            dma((H, C)),
            dma((H, C)),
            dma((H, C)),
            dma((H, C + 1)),
        ],
        compiler_params=pltpu.CompilerParams(collective_id=0, has_side_effects=True, vmem_limit_bytes=VMEM_LIMIT),
    )(tokens, norm_gain[None, :], gate_weight, up_weight, down_weight)


def solution(mesh):
    return jax.shard_map(
        functools.partial(on_device, mesh.shape["tensor"]),
        mesh=mesh,
        in_specs=(
            P(("dp", "tensor"), None),
            P(),
            P(None, "tensor"),
            P(None, "tensor"),
            P("tensor", None),
        ),
        out_specs=P("dp", "tensor"),
        check_vma=False,
    )
```

profile of v0, /device:TPU:0, one launch (start us, length us, event | category | flops | bytes accessed | tf_op | source)
XLA Modules:
  0.0 100.5 jit_solution(7771277016268494768)
XLA Ops:
  0.0 98.6 %shard_map.55 = bf16[512,512]{1,0:T(8,128)(2,1)} custom-call(bf16[64,4096]{1,0:T(8,128)(2,1)} %tok.1, f32[1,4096]{1,0:T(1,128)} %bitcast.1, bf16[4096,1792]{1,0:T(8,128)(2,1)} %gw.1, bf16[4096,1792]{1,0:T(8,128)(2,1)} %uw.1, bf16[1792,4096]{1,0:T(8,128)(2,1)} %dw.1), custom_call_target="tpu_custom_call" | custom-call | tf_op jit(solution)/shard_map/pallas_call | solution.py:249
  98.6 1.9 %copy.7 = bf16[512,512]{1,0:T(8,128)(2,1)} copy(bf16[512,512]{1,0:T(8,128)(2,1)} %shard_map.55) | data formatting | bytes 1048576
where the time goes:
time: 101 us; the launch traced here: 100 us
  Pallas kernels  98.6 us (98%)
  local copies, waits for them, and re-layouts  1.87 us (2%)
    pallas_call x1, Pallas kernels, on_device(): pl.pallas_call(functools.partial(block_kernel, n), out_shape=jax.ShapeDty...  98.6 us

commit v1 on v0

v1 whole, which is shorter than its diff:
```python
import functools

import jax
import jax.numpy as jnp
from jax import lax
from jax.experimental import pallas as pl
from jax.experimental.pallas import tpu as pltpu
from jax.sharding import PartitionSpec as P

SUBS = 2
VMEM_LIMIT = 67043328
f32, bf16 = jnp.float32, jnp.bfloat16


def tile_of(F):
    return next(t for t in (896, 512, 256, 128) if F % t == 0)


def block_kernel(
    n, tok, gain, gw, uw, dw, out,
    gwv, uwv, dwv, every, normed, hidden, mine, theirs, peer, arrived, far, acc,
    load_sem, own_sem, ag_recv, ag_send, peer_send, peer_recv, rs_send, rs_recv, far_recv,
):
    S = SUBS
    dp = lax.axis_index("dp")
    me = lax.axis_index("tensor")
    C = n // 2
    p, c = me // 2, me % 2
    R, D = tok.shape
    Rs = R // S
    T = 2 * R
    F = gwv.shape[1]
    W = D // n
    tile = tile_of(F)
    tiles = F // tile
    partner = (dp, 2 * p + (1 - c))
    right = (dp, lax.rem(me + 2, n))
    left = (dp, lax.rem(me + n - 2, n))
    first, last = (dp, c), (dp, 2 * (C - 1) + c)
    has_right, has_left = p < C - 1, p > 0
    leans_left = 2 * p < C - 1
    near = jnp.where(leans_left, -1, 1)
    both = jnp.where(leans_left, p, C - 1 - p)

    def rows_of(b, j, q):
        return pl.ds(pl.multiple_of(((b * S + j) * 2 + q) * Rs, Rs), Rs)

    def block_rows(b):
        return pl.ds(pl.multiple_of(b * T, T), T)

    def columns(t):
        return pl.ds(pl.multiple_of(t * W, W), W)

    own = [pltpu.make_async_copy(tok.at[pl.ds(j * Rs, Rs), :], every.at[rows_of(p, j, c), :], own_sem.at[j]) for j in range(S)]

    def load_tile(i):
        at = pl.ds(i * tile, tile)
        return (
            pltpu.make_async_copy(gw.at[:, at], gwv.at[:, at], load_sem.at[2 * i]),
            pltpu.make_async_copy(uw.at[:, at], uwv.at[:, at], load_sem.at[2 * i + 1]),
        )

    load_down = pltpu.make_async_copy(dw, dwv, load_sem.at[2 * tiles])

    for copy in own:
        copy.start()
    for i in range(tiles):
        for copy in load_tile(i):
            copy.start()

    barrier = pltpu.get_barrier_semaphore()

    def greet(device):
        pl.semaphore_signal(barrier, inc=1, device_id=device, device_id_type=pl.DeviceIdType.MESH)

    greet(partner)
    pl.when(has_right)(lambda: greet(right))
    pl.when(has_left)(lambda: greet(left))
    pl.when(p >= 2)(lambda: greet(first))
    pl.when(p <= C - 3)(lambda: greet(last))
    ends = (p == 0).astype(jnp.int32) + (p == C - 1).astype(jnp.int32)
    pl.semaphore_wait(barrier, 1 + has_right.astype(jnp.int32) + has_left.astype(jnp.int32) + ends * (C - 2))

    def remote(src, dst, s, d, device):
        return pltpu.make_async_remote_copy(
            src_ref=src, dst_ref=dst, send_sem=s, recv_sem=d, device_id=device, device_id_type=pl.DeviceIdType.MESH
        )

    def gather(b, j, way):
        at = every.at[rows_of(b, j, c), :]
        return remote(at, at, ag_send.at[way, b, j], ag_recv.at[b, j, c], (right, left, partner)[way])

    def gathered(b, j, q):
        at = every.at[rows_of(b, j, q), :]
        remote(at, at, ag_send.at[2, b, j], ag_recv.at[b, j, q], partner).wait_recv()

    def relay(k, j):
        @pl.when(p - k >= 0)
        def _():
            gathered(p - k, j, c)
            pl.when(has_right)(lambda: gather(p - k, j, 0).start())
            gather(p - k, j, 2).start()

        @pl.when(p + k <= C - 1)
        def _():
            gathered(p + k, j, c)
            pl.when(has_left)(lambda: gather(p + k, j, 1).start())
            gather(p + k, j, 2).start()

    def to_peer(b, d):
        return remote(theirs.at[b, d], peer.at[b, d], peer_send.at[b, d], peer_recv.at[b, d], partner)

    def to_right(b, d):
        return remote(mine.at[b, d], arrived.at[b, d + 1], rs_send.at[b, d], rs_recv.at[b, d + 1], right)

    def to_left(b, d):
        return remote(mine.at[b, d], arrived.at[b, d], rs_send.at[b, d], rs_recv.at[b, d], left)

    def to_far(side, b, d):
        return remote(mine.at[b, d], far.at[side], rs_send.at[b, d], far_recv.at[side], (dp, 2 * d + c))

    def landed(b, slot):
        remote(arrived.at[b, slot], arrived.at[b, slot], rs_send.at[b, 0], rs_recv.at[b, slot], partner).wait_recv()

    def landed_far(side):
        remote(far.at[side], far.at[side], rs_send.at[0, 0], far_recv.at[side], partner).wait_recv()

    def first_send(b, d):
        rightward, leftward = d > p, d < p
        straight = (p == 0) & (b == C - 1) & (d >= 2)
        pl.when(straight)(lambda: to_far(0, b, d).start())
        pl.when(rightward & ((p == 0) | ((p == 1) & (b == C - 1))) & jnp.logical_not(straight))(lambda: to_right(b, d).start())
        straight_left = (p == C - 1) & (b == 0) & (d <= C - 3)
        pl.when(straight_left)(lambda: to_far(1, b, d).start())
        pl.when(leftward & ((p == C - 1) | ((p == C - 2) & (b == 0))) & jnp.logical_not(straight_left))(lambda: to_left(b, d).start())

    def add_to_mine(b, d, slot):
        landed(b, slot)
        mine[b, d] = (mine[b, d].astype(f32) + arrived[b, slot].astype(f32)).astype(bf16)

    def forward_right(b):
        for i in range(C - 1):
            d = C - 1 - i

            @pl.when(d > p)
            def _():
                add_to_mine(b, d, d + 1)
                to_right(b, d).start()

    def forward_left(b):
        for d in range(C - 1):
            @pl.when(d < p)
            def _():
                add_to_mine(b, d, d)
                to_left(b, d).start()

    def early(b):
        pl.when((p == 1) & has_right)(lambda: forward_right(b))
        pl.when((p == C - 2) & has_left)(lambda: forward_left(C - 1 - b))

    def final(b):
        acc_b = acc.at[block_rows(b), :]

        @pl.when(has_left)
        def _():
            landed(b, p + 1)
            acc_b[...] += arrived[b, p + 1].astype(f32)

        @pl.when(has_right)
        def _():
            landed(b, p)
            acc_b[...] += arrived[b, p].astype(f32)

        @pl.when((b == C - 1) & (p >= 2))
        def _():
            landed_far(0)
            acc_b[...] += far[0].astype(f32)

        @pl.when((b == 0) & (p <= C - 3))
        def _():
            landed_far(1)
            acc_b[...] += far[1].astype(f32)

        for j in range(S):
            for q in range(2):
                at = pl.ds(pl.multiple_of((2 * b + q) * R + j * Rs, Rs), Rs)
                out[at, :] = acc[rows_of(b, j, q), :].astype(bf16)

    def norm(b):
        step = 32

        @pl.loop(0, T // step)
        def _(i):
            at = pl.ds(pl.multiple_of(b * T + i * step, step), step)
            wide = every[at, :].astype(f32)
            scale = 1.0 / jnp.sqrt(jnp.mean(wide * wide, axis=1, keepdims=True) + 1e-05)
            normed[pl.ds(pl.multiple_of(i * step, step), step), :] = (wide * gain[...] * scale).astype(bf16)

    def expand(s):
        @pl.loop(0, tiles)
        def _(i):
            @pl.when((s == 0) & (i == tiles - 1))
            def _():
                relay(1, 0)

            @pl.when(s == 0)
            def _():
                for x in range(tiles):
                    @pl.when(i == x)
                    def _():
                        for copy in load_tile(x):
                            copy.wait()

                pl.when(i == 0)(lambda: load_down.start())

            at = pl.ds(pl.multiple_of(i * tile, tile), tile)
            gate = jnp.dot(normed[...], gwv[:, at], preferred_element_type=f32)
            up = jnp.dot(normed[...], uwv[:, at], preferred_element_type=f32)
            hidden[:, at] = (jax.nn.silu(gate) * up).astype(bf16)

    def down(b):
        def dest(i):
            return jnp.where(leans_left, C - 1 - i, i)

        @pl.loop(0, C)
        def _(i):
            d = dest(i)
            theirs[b, d] = jnp.dot(hidden[...], dwv[:, columns(2 * d + 1 - c)], preferred_element_type=f32).astype(bf16)
            to_peer(b, d).start()

        @pl.loop(0, C)
        def _(i):
            d = dest(i)
            to_peer(b, d).wait_recv()
            total = jnp.dot(hidden[...], dwv[:, columns(2 * d + c)], preferred_element_type=f32) + peer[b, d].astype(f32)
            mine[b, d] = total.astype(bf16)

            @pl.when(d == p)
            def _():
                acc[block_rows(b), :] = every[block_rows(b), columns(me)].astype(f32) + mine[b, d].astype(f32)

            first_send(b, d)

    for j in range(S):
        own[j].wait()
        pl.when(has_right)(lambda: gather(p, j, 0).start())
        pl.when(has_left)(lambda: gather(p, j, 1).start())
        gather(p, j, 2).start()

    @pl.loop(0, C)
    def _(s):
        k = jnp.where(s <= 2 * both, (s + 1) // 2, s - both)
        side = jnp.where((s <= 2 * both) & (s % 2 == 1), near, -near)
        b = p + side * k

        pl.when((s >= 1) & (k == s))(lambda: relay(s, 1))
        for j in range(S):
            gathered(b, j, 1 - c)
        norm(b)
        expand(s)
        pl.when((s >= 1) & (k != s))(lambda: relay(s, 1))
        pl.when((s >= 1) & (s + 1 <= C - 1))(lambda: relay(s + 1, 0))
        pl.when(s >= 3)(lambda: early(s - 2))
        pl.when(s == 0)(lambda: load_down.wait())
        down(b)
        pl.when(s == 1)(lambda: early(0))

    order = [*range(C - 2), C - 1, C - 2]
    for b in order:
        passes = has_left & has_right & jnp.logical_not((p == 1) & ((b == C - 1) | (b <= C - 3)))
        pl.when(passes)(lambda: forward_right(b))
        passes = has_left & has_right & jnp.logical_not((p == C - 2) & ((b == C - 1) | (b <= C - 3)))
        pl.when(passes)(lambda: forward_left(C - 1 - b))
    for b in order:
        final(jnp.where(leans_left, C - 1 - b, b))

    for b in range(C):
        for j in range(S):
            pl.when((b <= p) & has_right)(lambda: gather(b, j, 0).wait_send())
            pl.when((b >= p) & has_left)(lambda: gather(b, j, 1).wait_send())
            gather(b, j, 2).wait_send()
        for d in range(C):
            to_peer(b, d).wait_send()
            pl.when(d != p)(lambda: to_right(b, d).wait_send())


def on_device(n, tokens, norm_gain, gate_weight, up_weight, down_weight):
    S = SUBS
    R, D = tokens.shape
    F = gate_weight.shape[1]
    C = n // 2
    T, W = 2 * R, D // n
    any_space, vmem = pl.BlockSpec(memory_space=pl.ANY), pl.BlockSpec(memory_space=pltpu.VMEM)
    dma = pltpu.SemaphoreType.DMA
    return pl.pallas_call(
        functools.partial(block_kernel, n),
        out_shape=jax.ShapeDtypeStruct((n * R, W), bf16),
        in_specs=[any_space, vmem, any_space, any_space, any_space],
        out_specs=vmem,
        scratch_shapes=[
            pltpu.VMEM((D, F), bf16),
            pltpu.VMEM((D, F), bf16),
            pltpu.VMEM((F, D), bf16),
            pltpu.VMEM((C * T, D), bf16),
            pltpu.VMEM((T, D), bf16),
            pltpu.VMEM((T, F), bf16),
            pltpu.VMEM((C, C, T, W), bf16),
            pltpu.VMEM((C, C, T, W), bf16),
            pltpu.VMEM((C, C, T, W), bf16),
            pltpu.VMEM((C, C + 1, T, W), bf16),
            pltpu.VMEM((2, T, W), bf16),
            pltpu.VMEM((C * T, W), f32),
            dma((2 * (F // tile_of(F)) + 1,)),
            dma((S,)),
            dma((C, S, 2)),
            dma((3, C, S)),
            dma((C, C)),
            dma((C, C)),
            dma((C, C)),
            dma((C, C + 1)),
            dma((2,)),
        ],
        compiler_params=pltpu.CompilerParams(collective_id=0, has_side_effects=True, vmem_limit_bytes=VMEM_LIMIT),
    )(tokens, norm_gain[None, :], gate_weight, up_weight, down_weight)


def solution(mesh):
    return jax.shard_map(
        functools.partial(on_device, mesh.shape["tensor"]),
        mesh=mesh,
        in_specs=(
            P(("dp", "tensor"), None),
            P(),
            P(None, "tensor"),
            P(None, "tensor"),
            P("tensor", None),
        ),
        out_specs=P("dp", "tensor"),
        check_vma=False,
    )
```

time: 101 us -> 83.6 us (0.83)
  Pallas kernels: 98.6 us -> 81.5 us
    pallas_call x1, Pallas kernels: 98.6 us -> 81.5 us  [on_device(): pl.pallas_call(functools.partial(block_kernel, n), out_shape=jax.ShapeDty...]
where the time goes in v1:
time: 83.6 us; the launch traced here: 83.4 us
  Pallas kernels  81.5 us (97%)
  local copies, waits for them, and re-layouts  1.87 us (2%)
    pallas_call x1, Pallas kernels, on_device(): pl.pallas_call(functools.partial(block_kernel, n), out_shape=jax.ShapeDty...  81.5 us
    unnamed x1, local copies, waits for them, and re-layouts  1.87 us

profile of v1, /device:TPU:0, one launch (start us, length us, event | category | flops | bytes accessed | tf_op | source)
XLA Modules:
  0.0 83.4 jit_solution(16685807868887095952)
XLA Ops:
  0.0 81.5 %shard_map.55 = bf16[512,512]{1,0:T(8,128)(2,1)} custom-call(bf16[64,4096]{1,0:T(8,128)(2,1)} %tok.1, f32[1,4096]{1,0:T(1,128)} %bitcast.1, bf16[4096,1792]{1,0:T(8,128)(2,1)} %gw.1, bf16[4096,1792]{1,0:T(8,128)(2,1)} %uw.1, bf16[1792,4096]{1,0:T(8,128)(2,1)} %dw.1), custom_call_target="tpu_custom_call" | custom-call | tf_op jit(solution)/shard_map/pallas_call | solution.py:295
  81.5 1.9 %copy.7 = bf16[512,512]{1,0:T(8,128)(2,1)} copy(bf16[512,512]{1,0:T(8,128)(2,1)} %shard_map.55) | data formatting | bytes 1048576

commit v2 on v1

v2 whole, which is shorter than its diff:
```python
import functools

import jax
import jax.numpy as jnp
from jax import lax
from jax.experimental import pallas as pl
from jax.experimental.pallas import tpu as pltpu
from jax.sharding import PartitionSpec as P

SUBS = 2
VMEM_LIMIT = 67043328
f32, bf16 = jnp.float32, jnp.bfloat16


def tile_of(F):
    return next(t for t in (256, 128) if F % t == 0)


def block_kernel(
    n, tok, gain, gw, uw, dw, out,
    gwv, uwv, dwv, every, normed, hidden, half, outv, mine, theirs, peer, arrived, far, acc,
    load_sem, own_sem, ag_recv, ag_send, peer_send, peer_recv, rs_send, rs_recv, far_recv, out_sem,
):
    S = SUBS
    dp = lax.axis_index("dp")
    me = lax.axis_index("tensor")
    C = n // 2
    p, c = me // 2, me % 2
    R, D = tok.shape
    Rs = R // S
    T = 2 * R
    F = gwv.shape[1]
    W = D // n
    tile = tile_of(F)
    tiles = F // tile
    cuts = [0, (tiles + 1) // 2, tiles]
    partner = (dp, 2 * p + (1 - c))
    right = (dp, lax.rem(me + 2, n))
    left = (dp, lax.rem(me + n - 2, n))
    has_right, has_left = p < C - 1, p > 0
    inner = has_right & has_left
    outer = jnp.logical_not(inner)
    leans_left = 2 * p < C - 1
    near = jnp.where(leans_left, -1, 1)
    both = jnp.where(leans_left, p, C - 1 - p)

    def rows_of(b, j, q):
        return pl.ds(pl.multiple_of(((b * S + j) * 2 + q) * Rs, Rs), Rs)

    def block_rows(b):
        return pl.ds(pl.multiple_of(b * T, T), T)

    def columns(t):
        return pl.ds(pl.multiple_of(t * W, W), W)

    own = [pltpu.make_async_copy(tok.at[pl.ds(j * Rs, Rs), :], every.at[rows_of(p, j, c), :], own_sem.at[j]) for j in range(S)]

    def load_wide(i):
        at = pl.ds(cuts[i] * tile, (cuts[i + 1] - cuts[i]) * tile)
        return (
            pltpu.make_async_copy(gw.at[:, at], gwv.at[:, at], load_sem.at[2 * i]),
            pltpu.make_async_copy(uw.at[:, at], uwv.at[:, at], load_sem.at[2 * i + 1]),
        )

    def load_down(q, d):
        return pltpu.make_async_copy(
            dw.at[:, columns(2 * d + q)], dwv.at[q, :, pl.ds(d * W, W)], load_sem.at[4 + C * q + d]
        )

    for copy in own:
        copy.start()

    barrier = pltpu.get_barrier_semaphore()

    def greet(device):
        pl.semaphore_signal(barrier, inc=1, device_id=device, device_id_type=pl.DeviceIdType.MESH)

    greet(partner)
    pl.when(has_right)(lambda: greet(right))
    pl.when(has_left)(lambda: greet(left))
    with jax.named_scope("own"):
        for copy in own:
            copy.wait()
    for i in range(2):
        for copy in load_wide(i):
            copy.start()
    with jax.named_scope("barrier"):
        pl.semaphore_wait(barrier, 1 + has_right.astype(jnp.int32) + has_left.astype(jnp.int32))

    def remote(src, dst, s, d, device):
        return pltpu.make_async_remote_copy(
            src_ref=src, dst_ref=dst, send_sem=s, recv_sem=d, device_id=device, device_id_type=pl.DeviceIdType.MESH
        )

    def gather(b, j, way):
        at = every.at[rows_of(b, j, c), :]
        return remote(at, at, ag_send.at[way, b, j], ag_recv.at[b, j, c], (right, left, partner)[way])

    def gathered(b, j, q):
        at = every.at[rows_of(b, j, q), :]
        remote(at, at, ag_send.at[2, b, j], ag_recv.at[b, j, q], partner).wait_recv()

    @jax.named_scope("relay")
    def relay(k, j):
        @pl.when(p - k >= 0)
        def _():
            gathered(p - k, j, c)
            pl.when(has_right)(lambda: gather(p - k, j, 0).start())
            gather(p - k, j, 2).start()

        @pl.when(p + k <= C - 1)
        def _():
            gathered(p + k, j, c)
            pl.when(has_left)(lambda: gather(p + k, j, 1).start())
            gather(p + k, j, 2).start()

    def to_peer(b, d):
        return remote(theirs.at[b, d], peer.at[b, d], peer_send.at[b, d], peer_recv.at[b, d], partner)

    def to_right(b, d):
        return remote(mine.at[b, d], arrived.at[b, d + 1], rs_send.at[b, d], rs_recv.at[b, d + 1], right)

    def to_left(b, d):
        return remote(mine.at[b, d], arrived.at[b, d], rs_send.at[b, d], rs_recv.at[b, d], left)

    def to_far(side, b, d):
        return remote(mine.at[b, d], far.at[side], rs_send.at[b, d], far_recv.at[side], (dp, 2 * d + c))

    def landed(b, slot):
        remote(arrived.at[b, slot], arrived.at[b, slot], rs_send.at[b, 0], rs_recv.at[b, slot], partner).wait_recv()

    def landed_far(side):
        remote(far.at[side], far.at[side], rs_send.at[0, 0], far_recv.at[side], partner).wait_recv()

    def straight_right(b, d):
        return (C > 2) & (b == C - 1) & (d == C - 1)

    def straight_left(b, d):
        return (C > 2) & (b == 0) & (d == 0)

    def first_send(b, d):
        straight = straight_right(b, d)
        pl.when((p == 0) & straight)(lambda: to_far(0, b, d).start())
        pl.when((d > p) & jnp.where(straight, p == 1, p == 0))(lambda: to_right(b, d).start())
        straight = straight_left(b, d)
        pl.when((p == C - 1) & straight)(lambda: to_far(1, b, d).start())
        pl.when((d < p) & jnp.where(straight, p == C - 2, p == C - 1))(lambda: to_left(b, d).start())

    def add_to_mine(b, d, slot):
        landed(b, slot)
        mine[b, d] = (mine[b, d].astype(f32) + arrived[b, slot].astype(f32)).astype(bf16)

    @jax.named_scope("right")
    def forward_right(b):
        for i in range(C - 1):
            d = C - 1 - i

            @pl.when((d > p) & jnp.logical_not((p == 1) & straight_right(b, d)))
            def _():
                add_to_mine(b, d, d + 1)
                to_right(b, d).start()

    @jax.named_scope("left")
    def forward_left(b):
        for d in range(C - 1):
            @pl.when((d < p) & jnp.logical_not((p == C - 2) & straight_left(b, d)))
            def _():
                add_to_mine(b, d, d)
                to_left(b, d).start()

    def early(b):
        pl.when((p == 1) & has_right)(lambda: forward_right(b))
        pl.when((p == C - 2) & has_left)(lambda: forward_left(C - 1 - b))

    def earlier():
        pl.when((p == 2) & has_right)(lambda: forward_right(1))
        pl.when((p == C - 3) & has_left)(lambda: forward_left(C - 2))

    @jax.named_scope("final")
    def final(b):
        acc_b = acc.at[block_rows(b), :]

        @pl.when(has_left)
        def _():
            landed(b, p + 1)
            acc_b[...] += arrived[b, p + 1].astype(f32)

        @pl.when(has_right)
        def _():
            landed(b, p)
            acc_b[...] += arrived[b, p].astype(f32)

        @pl.when(straight_right(b, p))
        def _():
            landed_far(0)
            acc_b[...] += far[0].astype(f32)

        @pl.when(straight_left(b, p))
        def _():
            landed_far(1)
            acc_b[...] += far[1].astype(f32)

        for j in range(S):
            for q in range(2):
                outv[b, pl.ds(q * R + j * Rs, Rs), :] = acc[rows_of(b, j, q), :].astype(bf16)

        store(b).start()

    def store(b):
        return pltpu.make_async_copy(outv.at[b], out.at[block_rows(b), :], out_sem.at[b])

    @jax.named_scope("norm")
    def norm(b):
        step = 32

        @pl.loop(0, T // step)
        def _(i):
            at = pl.ds(pl.multiple_of(b * T + i * step, step), step)
            wide = every[at, :].astype(f32)
            scale = 1.0 / jnp.sqrt(jnp.mean(wide * wide, axis=1, keepdims=True) + 1e-05)
            normed[pl.ds(pl.multiple_of(i * step, step), step), :] = (wide * gain[...] * scale).astype(bf16)

    def expand(s):
        def part(i):
            for x in range(cuts[i], cuts[i + 1]):
                at = pl.ds(x * tile, tile)
                gate = jnp.dot(normed[...], gwv[:, at], preferred_element_type=f32)
                up = jnp.dot(normed[...], uwv[:, at], preferred_element_type=f32)
                hidden[:, at] = (jax.nn.silu(gate) * up).astype(bf16)

        @pl.when(s == 0)
        def _():
            with jax.named_scope("load"):
                for copy in load_wide(0):
                    copy.wait()
                for q in range(2):
                    for d in range(C):
                        load_down(jnp.where(c == 0, 1 - q, q), d).start()

        with jax.named_scope("expand0"):
            part(0)
        pl.when(inner & (s <= 1))(lambda: relay(s + 1, 0))

        @pl.when(s == 0)
        def _():
            with jax.named_scope("load"):
                for copy in load_wide(1):
                    copy.wait()

        with jax.named_scope("expand1"):
            part(1)

    def down(b, s):
        def dest(i):
            return jnp.where(leans_left, C - 1 - i, i)

        def product(q, d):
            return jnp.dot(hidden[...], dwv[q, :, pl.ds(d * W, W)], preferred_element_type=f32)

        @pl.when(s == 0)
        def _():
            with jax.named_scope("load"):
                for d in range(C):
                    load_down(1 - c, d).wait()

        with jax.named_scope("down0"):
            for d in range(C):
                theirs[b, d] = product(1 - c, d).astype(bf16)
        for i in range(C):
            to_peer(b, dest(i)).start()

        pl.when(inner & (s <= 1))(lambda: relay(s + 1, 1))
        pl.when(s >= 2)(lambda: early(s - 1))

        @pl.when(s == 0)
        def _():
            with jax.named_scope("load"):
                for d in range(C):
                    load_down(c, d).wait()

        with jax.named_scope("down1"):
            for d in range(C):
                half[d] = product(c, d)
        for i in range(C):
            d = dest(i)
            with jax.named_scope("peer"):
                to_peer(b, d).wait_recv()
            mine[b, d] = (half[d] + peer[b, d].astype(f32)).astype(bf16)
            first_send(b, d)

        acc[block_rows(b), :] = every[block_rows(b), columns(me)].astype(f32) + mine[b, p].astype(f32)

    for j in range(S):
        pl.when(has_right)(lambda: gather(p, j, 0).start())
        pl.when(has_left)(lambda: gather(p, j, 1).start())
        gather(p, j, 2).start()

    @pl.loop(0, C)
    def _(s):
        k = jnp.where(s <= 2 * both, (s + 1) // 2, s - both)
        side = jnp.where((s <= 2 * both) & (s % 2 == 1), near, -near)
        b = p + side * k

        pl.when(outer & (s >= 1))(lambda: relay(s, 1))
        with jax.named_scope("await"):
            for j in range(S):
                gathered(b, j, 1 - c)
        norm(b)
        expand(s)
        pl.when(inner & (s >= 3))(lambda: relay(s, 1))
        pl.when((outer | (s >= 2)) & (s + 1 <= C - 1))(lambda: relay(s + 1, 0))
        pl.when(s == 3)(lambda: earlier())
        down(b, s)
        pl.when(s == 1)(lambda: early(0))

    late = C == 4
    for b in range(C):
        done = ((p == 1) & ((b <= C - 2) | late)) | ((p == 2) & (b == 1) & (C > 3))
        pl.when(inner & jnp.logical_not(done))(lambda: forward_right(b))
        done = ((p == C - 2) & ((b <= C - 2) | late)) | ((p == C - 3) & (b == 1) & (C > 3))
        pl.when(inner & jnp.logical_not(done))(lambda: forward_left(C - 1 - b))
    if late:
        pl.when(p == 1)(lambda: forward_right(C - 1))
        pl.when(p == C - 2)(lambda: forward_left(0))
    for b in range(C):
        final(jnp.where(leans_left, C - 1 - b, b))

    @jax.named_scope("drain")
    def drain(b):
        for j in range(S):
            pl.when((b <= p) & has_right)(lambda: gather(b, j, 0).wait_send())
            pl.when((b >= p) & has_left)(lambda: gather(b, j, 1).wait_send())
            gather(b, j, 2).wait_send()
        for d in range(C):
            to_peer(b, d).wait_send()
            pl.when(d != p)(lambda: to_right(b, d).wait_send())

    for b in range(C):
        drain(b)
    for b in range(C):
        store(b).wait()


def on_device(n, tokens, norm_gain, gate_weight, up_weight, down_weight):
    S = SUBS
    R, D = tokens.shape
    F = gate_weight.shape[1]
    C = n // 2
    T, W = 2 * R, D // n
    any_space, vmem = pl.BlockSpec(memory_space=pl.ANY), pl.BlockSpec(memory_space=pltpu.VMEM)
    dma = pltpu.SemaphoreType.DMA
    return pl.pallas_call(
        functools.partial(block_kernel, n),
        out_shape=jax.ShapeDtypeStruct((n * R, W), bf16),
        in_specs=[any_space, vmem, any_space, any_space, any_space],
        out_specs=any_space,
        scratch_shapes=[
            pltpu.VMEM((D, F), bf16),
            pltpu.VMEM((D, F), bf16),
            pltpu.VMEM((2, F, D // 2), bf16),
            pltpu.VMEM((C * T, D), bf16),
            pltpu.VMEM((T, D), bf16),
            pltpu.VMEM((T, F), bf16),
            pltpu.VMEM((C, T, W), f32),
            pltpu.VMEM((C, T, W), bf16),
            pltpu.VMEM((C, C, T, W), bf16),
            pltpu.VMEM((C, C, T, W), bf16),
            pltpu.VMEM((C, C, T, W), bf16),
            pltpu.VMEM((C, C + 1, T, W), bf16),
            pltpu.VMEM((2, T, W), bf16),
            pltpu.VMEM((C * T, W), f32),
            dma((4 + n,)),
            dma((S,)),
            dma((C, S, 2)),
            dma((3, C, S)),
            dma((C, C)),
            dma((C, C)),
            dma((C, C)),
            dma((C, C + 1)),
            dma((2,)),
            dma((C,)),
        ],
        compiler_params=pltpu.CompilerParams(collective_id=0, has_side_effects=True, vmem_limit_bytes=VMEM_LIMIT),
    )(tokens, norm_gain[None, :], gate_weight, up_weight, down_weight)


def solution(mesh):
    return jax.shard_map(
        functools.partial(on_device, mesh.shape["tensor"]),
        mesh=mesh,
        in_specs=(
            P(("dp", "tensor"), None),
            P(),
            P(None, "tensor"),
            P(None, "tensor"),
            P("tensor", None),
        ),
        out_specs=P("dp", "tensor"),
        check_vma=False,
    )
```

time: 83.6 us -> 65.2 us (0.78)
  Pallas kernels: 81.5 us -> 63.1 us
    pallas_call x1, Pallas kernels: 81.5 us -> 63.1 us  [on_device(): pl.pallas_call(functools.partial(block_kernel, n), out_shape=jax.ShapeDty...]
where the time goes in v2:
time: 65.2 us; the launch traced here: 64.9 us
  Pallas kernels  63.1 us (97%)
  local copies, waits for them, and re-layouts  1.87 us (3%)
    pallas_call x1, Pallas kernels, on_device(): pl.pallas_call(functools.partial(block_kernel, n), out_shape=jax.ShapeDty...  63.1 us
    unnamed x1, local copies, waits for them, and re-layouts  1.87 us

profile of v2, /device:TPU:0, one launch (start us, length us, event | category | flops | bytes accessed | tf_op | source)
XLA Modules:
  0.0 64.9 jit_solution(10279018623478186033)
XLA Ops:
  0.0 63.1 %shard_map.55 = bf16[512,512]{1,0:T(8,128)(2,1)} custom-call(bf16[64,4096]{1,0:T(8,128)(2,1)} %tok.1, f32[1,4096]{1,0:T(1,128)} %bitcast.1, bf16[4096,1792]{1,0:T(8,128)(2,1)} %gw.1, bf16[4096,1792]{1,0:T(8,128)(2,1)} %uw.1, bf16[1792,4096]{1,0:T(8,128)(2,1)} %dw.1), custom_call_target="tpu_custom_call" | custom-call | tf_op jit(solution)/shard_map/pallas_call | solution.py:352
  63.1 1.9 %copy.7 = bf16[512,512]{1,0:T(8,128)(2,1)} copy(bf16[512,512]{1,0:T(8,128)(2,1)} %shard_map.55) | data formatting | bytes 1048576

commit v3 on v2

--- a/solution.py
+++ b/solution.py
@@ -8,7 +8,7 @@
 from jax.sharding import PartitionSpec as P
 
 SUBS = 2
-VMEM_LIMIT = 67043328
+VMEM_LIMIT = 63963136
 f32, bf16 = jnp.float32, jnp.bfloat16
 
 
@@ -18,8 +18,8 @@
 
 def block_kernel(
     n, tok, gain, gw, uw, dw, out,
-    gwv, uwv, dwv, every, normed, hidden, half, outv, mine, theirs, peer, arrived, far, acc,
-    load_sem, own_sem, ag_recv, ag_send, peer_send, peer_recv, rs_send, rs_recv, far_recv, out_sem,
+    gwv, uwv, dwv, every, normed, hidden, half, mine, theirs, peer, arrived, far,
+    load_sem, own_sem, ag_recv, ag_send, peer_send, peer_recv, rs_send, rs_recv, far_recv,
 ):
     S = SUBS
     dp = lax.axis_index("dp")
@@ -39,7 +39,6 @@
     left = (dp, lax.rem(me + n - 2, n))
     has_right, has_left = p < C - 1, p > 0
     inner = has_right & has_left
-    outer = jnp.logical_not(inner)
     leans_left = 2 * p < C - 1
     near = jnp.where(leans_left, -1, 1)
     both = jnp.where(leans_left, p, C - 1 - p)
@@ -151,74 +150,66 @@
         mine[b, d] = (mine[b, d].astype(f32) + arrived[b, slot].astype(f32)).astype(bf16)
 
     @jax.named_scope("right")
-    def forward_right(b):
-        for i in range(C - 1):
-            d = C - 1 - i
-
+    def forward_right(b, targets=range(C - 1, 0, -1)):
+        for d in targets:
             @pl.when((d > p) & jnp.logical_not((p == 1) & straight_right(b, d)))
             def _():
                 add_to_mine(b, d, d + 1)
                 to_right(b, d).start()
 
     @jax.named_scope("left")
-    def forward_left(b):
-        for d in range(C - 1):
+    def forward_left(b, targets=range(C - 1)):
+        for d in targets:
             @pl.when((d < p) & jnp.logical_not((p == C - 2) & straight_left(b, d)))
             def _():
                 add_to_mine(b, d, d)
                 to_left(b, d).start()
 
-    def early(b):
-        pl.when((p == 1) & has_right)(lambda: forward_right(b))
-        pl.when((p == C - 2) & has_left)(lambda: forward_left(C - 1 - b))
+    def early(b, part):
+        ahead = slice(0, 1) if part == 0 else slice(1, None)
+        pl.when((p == 1) & has_right)(lambda: forward_right(b, range(C - 1, 0, -1)[ahead]))
+        pl.when((p == C - 2) & has_left)(lambda: forward_left(C - 1 - b, range(C - 1)[ahead]))
 
     def earlier():
         pl.when((p == 2) & has_right)(lambda: forward_right(1))
         pl.when((p == C - 3) & has_left)(lambda: forward_left(C - 2))
 
+    def pieces(b):
+        for j in range(S):
+            for q in range(2):
+                yield pl.ds((j * 2 + q) * Rs, Rs), rows_of(b, j, q), pl.ds(pl.multiple_of((2 * b + q) * R + j * Rs, Rs), Rs)
+
+    def add_to_out(b, ref):
+        for at, _, to in pieces(b):
+            out[to, :] += ref[at, :].astype(f32)
+
     @jax.named_scope("final")
     def final(b):
-        acc_b = acc.at[block_rows(b), :]
-
         @pl.when(has_left)
         def _():
             landed(b, p + 1)
-            acc_b[...] += arrived[b, p + 1].astype(f32)
+            add_to_out(b, arrived.at[b, p + 1])
 
         @pl.when(has_right)
         def _():
             landed(b, p)
-            acc_b[...] += arrived[b, p].astype(f32)
+            add_to_out(b, arrived.at[b, p])
 
         @pl.when(straight_right(b, p))
         def _():
             landed_far(0)
-            acc_b[...] += far[0].astype(f32)
+            add_to_out(b, far.at[0])
 
         @pl.when(straight_left(b, p))
         def _():
             landed_far(1)
-            acc_b[...] += far[1].astype(f32)
-
-        for j in range(S):
-            for q in range(2):
-                outv[b, pl.ds(q * R + j * Rs, Rs), :] = acc[rows_of(b, j, q), :].astype(bf16)
-
-        store(b).start()
-
-    def store(b):
-        return pltpu.make_async_copy(outv.at[b], out.at[block_rows(b), :], out_sem.at[b])
+            add_to_out(b, far.at[1])
 
     @jax.named_scope("norm")
-    def norm(b):
-        step = 32
-
-        @pl.loop(0, T // step)
-        def _(i):
-            at = pl.ds(pl.multiple_of(b * T + i * step, step), step)
-            wide = every[at, :].astype(f32)
-            scale = 1.0 / jnp.sqrt(jnp.mean(wide * wide, axis=1, keepdims=True) + 1e-05)
-            normed[pl.ds(pl.multiple_of(i * step, step), step), :] = (wide * gain[...] * scale).astype(bf16)
+    def norm(b, j, q):
+        wide = every[rows_of(b, j, q), :].astype(f32)
+        scale = 1.0 / jnp.sqrt(jnp.mean(wide * wide, axis=1, keepdims=True) + 1e-05)
+        normed[rows_of(0, j, q), :] = (wide * gain[...] * scale).astype(bf16)
 
     def expand(s):
         def part(i):
@@ -239,7 +230,6 @@
 
         with jax.named_scope("expand0"):
             part(0)
-        pl.when(inner & (s <= 1))(lambda: relay(s + 1, 0))
 
         @pl.when(s == 0)
         def _():
@@ -251,11 +241,14 @@
             part(1)
 
     def down(b, s):
+        far_block = jnp.where(leans_left, (p == 0) & (b == C - 1), (p == C - 1) & (b == 0)) & (C > 2)
+
         def dest(i):
+            i = jnp.where(far_block, 1 - i, i) if i < 2 else i
             return jnp.where(leans_left, C - 1 - i, i)
 
         def product(q, d):
-            return jnp.dot(hidden[...], dwv[q, :, pl.ds(d * W, W)], preferred_element_type=f32)
+            return jnp.dot(hidden[...], dwv[q, :, pl.ds(pl.multiple_of(d * W, W), W)], preferred_element_type=f32)
 
         @pl.when(s == 0)
         def _():
@@ -263,14 +256,26 @@
                 for d in range(C):
                     load_down(1 - c, d).wait()
 
-        with jax.named_scope("down0"):
-            for d in range(C):
-                theirs[b, d] = product(1 - c, d).astype(bf16)
-        for i in range(C):
-            to_peer(b, dest(i)).start()
-
-        pl.when(inner & (s <= 1))(lambda: relay(s + 1, 1))
-        pl.when(s >= 2)(lambda: early(s - 1))
+        def give(at):
+            with jax.named_scope("down0"):
+                for i in at:
+                    theirs[b, dest(i)] = product(1 - c, dest(i)).astype(bf16)
+            for i in at:
+                to_peer(b, dest(i)).start()
+
+        def take(at):
+            with jax.named_scope("down1"):
+                for i in at:
+                    half[dest(i)] = product(c, dest(i))
+            for i in at:
+                d = dest(i)
+                with jax.named_scope("peer"):
+                    to_peer(b, d).wait_recv()
+                mine[b, d] = (half[d] + peer[b, d].astype(f32)).astype(bf16)
+                first_send(b, d)
+
+        give(range(1))
+        give(range(1, C))
 
         @pl.when(s == 0)
         def _():
@@ -278,17 +283,11 @@
                 for d in range(C):
                     load_down(c, d).wait()
 
-        with jax.named_scope("down1"):
-            for d in range(C):
-                half[d] = product(c, d)
-        for i in range(C):
-            d = dest(i)
-            with jax.named_scope("peer"):
-                to_peer(b, d).wait_recv()
-            mine[b, d] = (half[d] + peer[b, d].astype(f32)).astype(bf16)
-            first_send(b, d)
-
-        acc[block_rows(b), :] = every[block_rows(b), columns(me)].astype(f32) + mine[b, p].astype(f32)
+        take(range(1))
+        take(range(1, C))
+
+        for at, rows, to in pieces(b):
+            out[to, :] = every[rows, columns(me)].astype(f32) + mine[b, p, at, :].astype(f32)
 
     for j in range(S):
         pl.when(has_right)(lambda: gather(p, j, 0).start())
@@ -301,17 +300,25 @@
         side = jnp.where((s <= 2 * both) & (s % 2 == 1), near, -near)
         b = p + side * k
 
-        pl.when(outer & (s >= 1))(lambda: relay(s, 1))
-        with jax.named_scope("await"):
-            for j in range(S):
+        def other(j):
+            with jax.named_scope("await"):
                 gathered(b, j, 1 - c)
-        norm(b)
+
+        for j in range(S - 1):
+            other(j)
+            for q in range(2):
+                norm(b, j, q)
+        pl.when(s >= 1)(lambda: relay(s, S - 1))
+        norm(b, S - 1, c)
+        other(S - 1)
+        norm(b, S - 1, 1 - c)
         expand(s)
-        pl.when(inner & (s >= 3))(lambda: relay(s, 1))
-        pl.when((outer | (s >= 2)) & (s + 1 <= C - 1))(lambda: relay(s + 1, 0))
+        pl.when(s + 1 <= C - 1)(lambda: relay(s + 1, 0))
+        pl.when(s >= 2)(lambda: early(s - 1, 0))
         pl.when(s == 3)(lambda: earlier())
         down(b, s)
-        pl.when(s == 1)(lambda: early(0))
+        pl.when(s == 1)(lambda: early(0, 0))
+        pl.when((s >= 1) & (s <= C - 2))(lambda: early(s - 1, 1))
 
     late = C == 4
     for b in range(C):
@@ -319,6 +326,8 @@
         pl.when(inner & jnp.logical_not(done))(lambda: forward_right(b))
         done = ((p == C - 2) & ((b <= C - 2) | late)) | ((p == C - 3) & (b == 1) & (C > 3))
         pl.when(inner & jnp.logical_not(done))(lambda: forward_left(C - 1 - b))
+        if b == 0:
+            early(C - 2, 1)
     if late:
         pl.when(p == 1)(lambda: forward_right(C - 1))
         pl.when(p == C - 2)(lambda: forward_left(0))
@@ -337,8 +346,6 @@
 
     for b in range(C):
         drain(b)
-    for b in range(C):
-        store(b).wait()
 
 
 def on_device(n, tokens, norm_gain, gate_weight, up_weight, down_weight):
@@ -349,11 +356,11 @@
     T, W = 2 * R, D // n
     any_space, vmem = pl.BlockSpec(memory_space=pl.ANY), pl.BlockSpec(memory_space=pltpu.VMEM)
     dma = pltpu.SemaphoreType.DMA
-    return pl.pallas_call(
+    mixed = pl.pallas_call(
         functools.partial(block_kernel, n),
-        out_shape=jax.ShapeDtypeStruct((n * R, W), bf16),
+        out_shape=pltpu.VMEM((n * R, W), f32),
         in_specs=[any_space, vmem, any_space, any_space, any_space],
-        out_specs=any_space,
+        out_specs=vmem,
         scratch_shapes=[
             pltpu.VMEM((D, F), bf16),
             pltpu.VMEM((D, F), bf16),
@@ -362,13 +369,11 @@
             pltpu.VMEM((T, D), bf16),
             pltpu.VMEM((T, F), bf16),
             pltpu.VMEM((C, T, W), f32),
-            pltpu.VMEM((C, T, W), bf16),
             pltpu.VMEM((C, C, T, W), bf16),
             pltpu.VMEM((C, C, T, W), bf16),
             pltpu.VMEM((C, C, T, W), bf16),
             pltpu.VMEM((C, C + 1, T, W), bf16),
             pltpu.VMEM((2, T, W), bf16),
-            pltpu.VMEM((C * T, W), f32),
             dma((4 + n,)),
             dma((S,)),
             dma((C, S, 2)),
@@ -378,10 +383,10 @@
             dma((C, C)),
             dma((C, C + 1)),
             dma((2,)),
-            dma((C,)),
         ],
         compiler_params=pltpu.CompilerParams(collective_id=0, has_side_effects=True, vmem_limit_bytes=VMEM_LIMIT),
     )(tokens, norm_gain[None, :], gate_weight, up_weight, down_weight)
+    return mixed.astype(bf16)
 
 
 def solution(mesh):

time: 65.2 us -> 60.4 us (0.926)
  Pallas kernels: 63.1 us -> 59.3 us
  local copies, waits for them, and re-layouts: 1.87 us -> 0 us
  other arithmetic: 0 us -> 0.86 us
    pallas_call x1, Pallas kernels: 63.1 us -> 59.3 us  [on_device(): pl.pallas_call(functools.partial(block_kernel, n), out_shape=pltpu.VMEM((...]
    unnamed x1 -> x0, local copies, waits for them, and re-layouts: 1.87 us -> none
    convert_element_type x0 -> x1, other arithmetic: none -> 0.86 us  [on_device(): return mixed.astype(bf16)]
where the time goes in v3:
time: 60.4 us; the launch traced here: 60.2 us
  Pallas kernels  59.3 us (98%)
  other arithmetic  0.86 us (1%)
    pallas_call x1, Pallas kernels, on_device(): pl.pallas_call(functools.partial(block_kernel, n), out_shape=pltpu.VMEM((...  59.3 us

profile of v3, /device:TPU:0, one launch (start us, length us, event | category | flops | bytes accessed | tf_op | source)
XLA Modules:
  0.0 60.2 jit_solution(12552575563048936819)
XLA Ops:
  0.0 59.3 %shard_map.55 = f32[512,512]{1,0:T(8,128)S(1)} custom-call(bf16[64,4096]{1,0:T(8,128)(2,1)} %tok.1, f32[1,4096]{1,0:T(1,128)} %bitcast.1, bf16[4096,1792]{1,0:T(8,128)(2,1)} %gw.1, bf16[4096,1792]{1,0:T(8,128)(2,1)} %uw.1, bf16[1792,4096]{1,0:T(8,128)(2,1)} %dw.1), custom_call_target="tpu_custom_call" | custom-call | tf_op jit(solution)/shard_map/pallas_call | solution.py:359
  59.3 0.9 %convert_element_type.3 = bf16[512,512]{1,0:T(8,128)(2,1)} convert(f32[512,512]{1,0:T(8,128)S(1)} %shard_map.55) | non-fusion elementwise | flops 262144 | bytes 1572864 | tf_op jit(solution)/shard_map/convert_element_type | solution.py:389

commit v4 on v3

v4 whole, which is shorter than its diff:
```python
import functools

import jax
import jax.numpy as jnp
from jax import lax
from jax.experimental import pallas as pl
from jax.experimental.pallas import tpu as pltpu
from jax.sharding import PartitionSpec as P

SUBS = 2
VMEM_LIMIT = 63963136
f32, bf16 = jnp.float32, jnp.bfloat16


def tile_of(F):
    return next(t for t in (256, 128) if F % t == 0)


def block_kernel(
    n, tok, gain, gw, uw, dw, out,
    wide, dwv, gainv, every, normed, hidden, other, half, mine, arrived, far,
    load_sem, own_sem, ag_recv, ag_send, pair_send, pair_recv, down_send, down_recv, rs_send, rs_recv, far_recv,
):
    S = SUBS
    dp = lax.axis_index("dp")
    me = lax.axis_index("tensor")
    C = n // 2
    p, c = me // 2, me % 2
    R, D = tok.shape
    Rs = R // S
    T = 2 * R
    F = wide.shape[2]
    W = D // n
    tile = tile_of(F)
    tiles = F // tile
    cuts = [0, (tiles + 1) // 2, tiles]
    partner = (dp, 2 * p + (1 - c))
    right = (dp, lax.rem(me + 2, n))
    left = (dp, lax.rem(me + n - 2, n))
    has_right, has_left = p < C - 1, p > 0
    inner = has_right & has_left
    leans_left = 2 * p < C - 1
    near = jnp.where(leans_left, -1, 1)
    both = jnp.where(leans_left, p, C - 1 - p)

    def rows_of(b, j, q):
        return pl.ds(pl.multiple_of(((b * S + j) * 2 + q) * Rs, Rs), Rs)

    def block_rows(b):
        return pl.ds(pl.multiple_of(b * T, T), T)

    def columns(t):
        return pl.ds(pl.multiple_of(t * W, W), W)

    own = [pltpu.make_async_copy(tok.at[pl.ds(j * Rs, Rs), :], every.at[rows_of(p, j, c), :], own_sem.at[0]) for j in range(S)]
    gain_copy = pltpu.make_async_copy(gain, gainv, own_sem.at[1])

    def load_wide(i):
        at = pl.ds(cuts[i] * tile, (cuts[i + 1] - cuts[i]) * tile)
        return [pltpu.make_async_copy((gw, uw)[x].at[:, at], wide.at[x, :, at], load_sem.at[i]) for x in range(2)]

    def load_down(d):
        return pltpu.make_async_copy(dw.at[:, columns(2 * d + c)], dwv.at[0, :, pl.ds(d * W, W)], load_sem.at[2])

    def all_of(ref, sem):
        pltpu.make_async_copy(ref, ref, sem).wait()

    def wide_loaded(i):
        all_of(wide.at[:, :, pl.ds(cuts[i] * tile, (cuts[i + 1] - cuts[i]) * tile)], load_sem.at[i])

    for copy in own:
        copy.start()
    gain_copy.start()

    barrier = pltpu.get_barrier_semaphore()

    def greet(device):
        pl.semaphore_signal(barrier, inc=1, device_id=device, device_id_type=pl.DeviceIdType.MESH)

    greet(partner)
    pl.when(has_right)(lambda: greet(right))
    pl.when(has_left)(lambda: greet(left))
    with jax.named_scope("own"):
        all_of(every.at[pl.ds(0, R), :], own_sem.at[0])
    for i in range(2):
        for copy in load_wide(i):
            copy.start()
    with jax.named_scope("barrier"):
        pl.semaphore_wait(barrier, 1 + has_right.astype(jnp.int32) + has_left.astype(jnp.int32))

    def remote(src, dst, s, d, device):
        return pltpu.make_async_remote_copy(
            src_ref=src, dst_ref=dst, send_sem=s, recv_sem=d, device_id=device, device_id_type=pl.DeviceIdType.MESH
        )

    def gather(b, j, way):
        at = every.at[rows_of(b, j, c), :]
        return remote(at, at, ag_send.at[way], ag_recv.at[b, j, c], (right, left, partner)[way])

    def gathered(b, j, q):
        at = every.at[rows_of(b, j, q), :]
        remote(at, at, ag_send.at[2], ag_recv.at[b, j, q], partner).wait_recv()

    @jax.named_scope("relay")
    def relay(k, j):
        @pl.when(p - k >= 0)
        def _():
            gathered(p - k, j, c)
            pl.when(has_right)(lambda: gather(p - k, j, 0).start())
            gather(p - k, j, 2).start()

        @pl.when(p + k <= C - 1)
        def _():
            gathered(p + k, j, c)
            pl.when(has_left)(lambda: gather(p + k, j, 1).start())
            gather(p + k, j, 2).start()

    def share_down(d):
        return remote(dw.at[:, columns(2 * d + 1 - c)], dwv.at[1, :, pl.ds(d * W, W)], down_send, down_recv, partner)

    def share_hidden(s, i):
        at = pl.ds(cuts[i] * tile, (cuts[i + 1] - cuts[i]) * tile)
        return remote(hidden.at[s % 2, :, at], other.at[s % 2, :, at], pair_send, pair_recv.at[s % 2, i], partner)

    def to_right(b, d):
        return remote(mine.at[b, d], arrived.at[b, d + 1], rs_send, rs_recv.at[b, d + 1], right)

    def to_left(b, d):
        return remote(mine.at[b, d], arrived.at[b, d], rs_send, rs_recv.at[b, d], left)

    def to_far(b, d):
        return remote(mine.at[b, d], far, rs_send, far_recv, (dp, 2 * d + c))

    def landed(b, slot):
        remote(arrived.at[b, slot], arrived.at[b, slot], rs_send, rs_recv.at[b, slot], partner).wait_recv()

    def landed_far():
        remote(far, far, rs_send, far_recv, partner).wait_recv()

    def straight_right(b, d):
        return (C > 2) & (b == C - 1) & (d == C - 1)

    def straight_left(b, d):
        return (C > 2) & (b == 0) & (d == 0)

    def first_send(b, d):
        straight = straight_right(b, d)
        pl.when((p == 0) & straight)(lambda: to_far(b, d).start())
        pl.when((d > p) & jnp.where(straight, p == 1, p == 0))(lambda: to_right(b, d).start())
        straight = straight_left(b, d)
        pl.when((p == C - 1) & straight)(lambda: to_far(b, d).start())
        pl.when((d < p) & jnp.where(straight, p == C - 2, p == C - 1))(lambda: to_left(b, d).start())

    def add_to_mine(b, d, slot):
        landed(b, slot)
        mine[b, d] = (mine[b, d].astype(f32) + arrived[b, slot].astype(f32)).astype(bf16)

    @jax.named_scope("right")
    def forward_right(b, targets=range(C - 1, 0, -1)):
        for d in targets:
            @pl.when((d > p) & jnp.logical_not((p == 1) & straight_right(b, d)))
            def _():
                add_to_mine(b, d, d + 1)
                to_right(b, d).start()

    @jax.named_scope("left")
    def forward_left(b, targets=range(C - 1)):
        for d in targets:
            @pl.when((d < p) & jnp.logical_not((p == C - 2) & straight_left(b, d)))
            def _():
                add_to_mine(b, d, d)
                to_left(b, d).start()

    def early(b, part):
        ahead = slice(0, 1) if part == 0 else slice(1, None)
        pl.when((p == 1) & has_right)(lambda: forward_right(b, range(C - 1, 0, -1)[ahead]))
        pl.when((p == C - 2) & has_left)(lambda: forward_left(C - 1 - b, range(C - 1)[ahead]))

    def earlier():
        pl.when((p == 2) & has_right)(lambda: forward_right(1))
        pl.when((p == C - 3) & has_left)(lambda: forward_left(C - 2))

    def pieces(b):
        for j in range(S):
            for q in range(2):
                yield pl.ds((j * 2 + q) * Rs, Rs), rows_of(b, j, q), pl.ds(pl.multiple_of((2 * b + q) * R + j * Rs, Rs), Rs)

    def add_to_out(b, ref):
        for at, _, to in pieces(b):
            out[to, :] += ref[at, :].astype(f32)

    @jax.named_scope("final")
    def final(b):
        @pl.when(has_left)
        def _():
            landed(b, p + 1)
            add_to_out(b, arrived.at[b, p + 1])

        @pl.when(has_right)
        def _():
            landed(b, p)
            add_to_out(b, arrived.at[b, p])

        @pl.when(straight_right(b, p) | straight_left(b, p))
        def _():
            landed_far()
            add_to_out(b, far)

    @jax.named_scope("norm")
    def norm(b, j, q):
        rows = every[rows_of(b, j, q), :].astype(f32)
        scale = 1.0 / jnp.sqrt(jnp.mean(rows * rows, axis=1, keepdims=True) + 1e-05)
        normed[rows_of(0, j, q), :] = (rows * gainv[...] * scale).astype(bf16)

    def expand(s):
        def part(i):
            for x in range(cuts[i], cuts[i + 1]):
                at = pl.ds(x * tile, tile)
                gate = jnp.dot(normed[...], wide[0, :, at], preferred_element_type=f32)
                up = jnp.dot(normed[...], wide[1, :, at], preferred_element_type=f32)
                hidden[s % 2, :, at] = (jax.nn.silu(gate) * up).astype(bf16)

        @pl.when(s == 0)
        def _():
            with jax.named_scope("load"):
                wide_loaded(0)
                for d in range(C):
                    load_down(d).start()

        with jax.named_scope("expand0"):
            part(0)
        share_hidden(s, 0).start()

        @pl.when(s == 0)
        def _():
            with jax.named_scope("load"):
                wide_loaded(1)

        with jax.named_scope("expand1"):
            part(1)
        share_hidden(s, 1).start()

    def down(b, s):
        far_block = jnp.where(leans_left, (p == 0) & (b == C - 1), (p == C - 1) & (b == 0)) & (C > 2)

        def dest(i):
            i = jnp.where(far_block, 1 - i, i) if i < 2 else i
            return jnp.where(leans_left, C - 1 - i, i)

        def product(of, x, d):
            weight = dwv[x, :, pl.ds(pl.multiple_of(d * W, W), W)]
            return jnp.dot(of[s % 2], weight, preferred_element_type=f32)

        @pl.when(s == 0)
        def _():
            with jax.named_scope("load"):
                all_of(dwv.at[0], load_sem.at[2])

        with jax.named_scope("down0"):
            for d in range(C):
                half[d] = product(hidden, 0, d)

        @pl.when(s == 0)
        def _():
            with jax.named_scope("load"):
                remote(dwv.at[1], dwv.at[1], down_send, down_recv, partner).wait_recv()

        with jax.named_scope("peer"):
            for i in range(2):
                share_hidden(s, i).wait_recv()
        for at in (range(1), range(1, C)):
            with jax.named_scope("down1"):
                for i in at:
                    d = dest(i)
                    mine[b, d] = (half[d] + product(other, 1, d)).astype(bf16)
            for i in at:
                first_send(b, dest(i))
        all_of(hidden.at[s % 2], pair_send)

        for at, rows, to in pieces(b):
            out[to, :] = every[rows, columns(me)].astype(f32) + mine[b, p, at, :].astype(f32)

    for j in range(S):
        pl.when(has_right)(lambda: gather(p, j, 0).start())
        pl.when(has_left)(lambda: gather(p, j, 1).start())
        gather(p, j, 2).start()
    for d in range(C):
        share_down(d).start()

    @pl.loop(0, C)
    def _(s):
        k = jnp.where(s <= 2 * both, (s + 1) // 2, s - both)
        side = jnp.where((s <= 2 * both) & (s % 2 == 1), near, -near)
        b = p + side * k

        def other(j):
            with jax.named_scope("await"):
                gathered(b, j, 1 - c)

        for j in range(S - 1):
            other(j)
            if j == 0:
                pl.when(s == 0)(lambda: gain_copy.wait())
            for q in range(2):
                norm(b, j, q)
        pl.when(s >= 1)(lambda: relay(s, S - 1))
        norm(b, S - 1, c)
        other(S - 1)
        norm(b, S - 1, 1 - c)
        expand(s)
        pl.when(s + 1 <= C - 1)(lambda: relay(s + 1, 0))
        pl.when(s >= 2)(lambda: early(s - 1, 0))
        pl.when(s == 3)(lambda: earlier())
        down(b, s)
        pl.when(s == 1)(lambda: early(0, 0))
        pl.when((s >= 1) & (s <= C - 2))(lambda: early(s - 1, 1))

    late = C == 4
    for b in range(C):
        done = ((p == 1) & ((b <= C - 2) | late)) | ((p == 2) & (b == 1) & (C > 3))
        pl.when(inner & jnp.logical_not(done))(lambda: forward_right(b))
        done = ((p == C - 2) & ((b <= C - 2) | late)) | ((p == C - 3) & (b == 1) & (C > 3))
        pl.when(inner & jnp.logical_not(done))(lambda: forward_left(C - 1 - b))
        if b == 0:
            early(C - 2, 1)
    if late:
        pl.when(p == 1)(lambda: forward_right(C - 1))
        pl.when(p == C - 2)(lambda: forward_left(0))
    for b in range(C):
        final(jnp.where(leans_left, C - 1 - b, b))

    with jax.named_scope("drain"):
        for x in range(C):
            pl.when((p == x) & has_right)(lambda: all_of(every.at[pl.ds(0, (x + 1) * R), :], ag_send.at[0]))
            pl.when((p == x) & has_left)(lambda: all_of(every.at[pl.ds(0, (C - x) * R), :], ag_send.at[1]))
        all_of(every.at[pl.ds(0, C * R), :], ag_send.at[2])
        all_of(dwv.at[1], down_send)
        all_of(mine.at[:, pl.ds(0, C - 1)], rs_send)


def on_device(n, tokens, norm_gain, gate_weight, up_weight, down_weight):
    S = SUBS
    R, D = tokens.shape
    F = gate_weight.shape[1]
    C = n // 2
    T, W = 2 * R, D // n
    any_space, vmem = pl.BlockSpec(memory_space=pl.ANY), pl.BlockSpec(memory_space=pltpu.VMEM)
    dma = pltpu.SemaphoreType.DMA
    mixed = pl.pallas_call(
        functools.partial(block_kernel, n),
        out_shape=pltpu.VMEM((n * R, W), f32),
        in_specs=[any_space] * 5,
        out_specs=vmem,
        scratch_shapes=[
            pltpu.VMEM((2, D, F), bf16),
            pltpu.VMEM((2, F, D // 2), bf16),
            pltpu.VMEM((1, D), f32),
            pltpu.VMEM((C * T, D), bf16),
            pltpu.VMEM((T, D), bf16),
            pltpu.VMEM((2, T, F), bf16),
            pltpu.VMEM((2, T, F), bf16),
            pltpu.VMEM((C, T, W), f32),
            pltpu.VMEM((C, C, T, W), bf16),
            pltpu.VMEM((C, C + 1, T, W), bf16),
            pltpu.VMEM((T, W), bf16),
            dma((3,)),
            dma((2,)),
            dma((C, S, 2)),
            dma((3,)),
            dma,
            dma((2, 2)),
            dma,
            dma,
            dma,
            dma((C, C + 1)),
            dma,
        ],
        compiler_params=pltpu.CompilerParams(collective_id=0, has_side_effects=True, vmem_limit_bytes=VMEM_LIMIT),
    )(tokens, norm_gain[None, :], gate_weight, up_weight, down_weight)
    return mixed.astype(bf16)


def solution(mesh):
    return jax.shard_map(
        functools.partial(on_device, mesh.shape["tensor"]),
        mesh=mesh,
        in_specs=(
            P(("dp", "tensor"), None),
            P(),
            P(None, "tensor"),
            P(None, "tensor"),
            P("tensor", None),
        ),
        out_specs=P("dp", "tensor"),
        check_vma=False,
    )
```

time: 60.4 us -> 58 us (0.960)
  Pallas kernels: 59.3 us -> 57 us
    pallas_call x1, Pallas kernels: 59.3 us -> 57 us  [on_device(): pl.pallas_call(functools.partial(block_kernel, n), out_shape=pltpu.VMEM((...]
where the time goes in v4:
time: 58 us; the launch traced here: 57.9 us
  Pallas kernels  57 us (98%)
  other arithmetic  0.86 us (1%)
    pallas_call x1, Pallas kernels, on_device(): pl.pallas_call(functools.partial(block_kernel, n), out_shape=pltpu.VMEM((...  57 us

profile of v4, /device:TPU:0, one launch (start us, length us, event | category | flops | bytes accessed | tf_op | source)
XLA Modules:
  0.0 57.9 jit_solution(15336889916859643364)
XLA Ops:
  0.0 57.0 %shard_map.55 = f32[512,512]{1,0:T(8,128)S(1)} custom-call(bf16[64,4096]{1,0:T(8,128)(2,1)} %tok.1, f32[1,4096]{1,0:T(1,128)} %bitcast.1, bf16[4096,1792]{1,0:T(8,128)(2,1)} %gw.1, bf16[4096,1792]{1,0:T(8,128)(2,1)} %uw.1, bf16[1792,4096]{1,0:T(8,128)(2,1)} %dw.1), custom_call_target="tpu_custom_call" | custom-call | tf_op jit(solution)/shard_map/pallas_call | solution.py:349
  57.0 0.9 %convert_element_type.3 = bf16[512,512]{1,0:T(8,128)(2,1)} convert(f32[512,512]{1,0:T(8,128)S(1)} %shard_map.55) | non-fusion elementwise | flops 262144 | bytes 1572864 | tf_op jit(solution)/shard_map/convert_element_type | solution.py:380

commit v5 on v4

--- a/solution.py
+++ b/solution.py
@@ -18,7 +18,7 @@
 
 def block_kernel(
     n, tok, gain, gw, uw, dw, out,
-    wide, dwv, gainv, every, normed, hidden, other, half, mine, arrived, far,
+    wide, dwv, gainv, every, normed, sums, partial, hidden, other, half, mine, arrived, far, acc,
     load_sem, own_sem, ag_recv, ag_send, pair_send, pair_recv, down_send, down_recv, rs_send, rs_recv, far_recv,
 ):
     S = SUBS
@@ -27,7 +27,7 @@
     C = n // 2
     p, c = me // 2, me % 2
     R, D = tok.shape
-    Rs = R // S
+    Dc = D // S
     T = 2 * R
     F = wide.shape[2]
     W = D // n
@@ -39,12 +39,17 @@
     left = (dp, lax.rem(me + n - 2, n))
     has_right, has_left = p < C - 1, p > 0
     inner = has_right & has_left
+    outer = jnp.logical_not(inner)
+    late = C == 4
     leans_left = 2 * p < C - 1
     near = jnp.where(leans_left, -1, 1)
     both = jnp.where(leans_left, p, C - 1 - p)
 
-    def rows_of(b, j, q):
-        return pl.ds(pl.multiple_of(((b * S + j) * 2 + q) * Rs, Rs), Rs)
+    def rows_of(b, q):
+        return pl.ds(pl.multiple_of((b * 2 + q) * R, R), R)
+
+    def features(j):
+        return pl.ds(j * Dc, Dc)
 
     def block_rows(b):
         return pl.ds(pl.multiple_of(b * T, T), T)
@@ -52,21 +57,20 @@
     def columns(t):
         return pl.ds(pl.multiple_of(t * W, W), W)
 
-    own = [pltpu.make_async_copy(tok.at[pl.ds(j * Rs, Rs), :], every.at[rows_of(p, j, c), :], own_sem.at[0]) for j in range(S)]
+    own = [pltpu.make_async_copy(tok.at[:, features(j)], every.at[rows_of(p, c), features(j)], own_sem.at[0]) for j in range(S)]
     gain_copy = pltpu.make_async_copy(gain, gainv, own_sem.at[1])
 
-    def load_wide(i):
-        at = pl.ds(cuts[i] * tile, (cuts[i + 1] - cuts[i]) * tile)
-        return [pltpu.make_async_copy((gw, uw)[x].at[:, at], wide.at[x, :, at], load_sem.at[i]) for x in range(2)]
+    def load_wide(j):
+        return [pltpu.make_async_copy((gw, uw)[x].at[features(j), :], wide.at[x, features(j), :], load_sem.at[j]) for x in range(2)]
 
     def load_down(d):
-        return pltpu.make_async_copy(dw.at[:, columns(2 * d + c)], dwv.at[0, :, pl.ds(d * W, W)], load_sem.at[2])
+        return pltpu.make_async_copy(dw.at[:, columns(2 * d + c)], dwv.at[0, :, pl.ds(d * W, W)], load_sem.at[S])
 
     def all_of(ref, sem):
         pltpu.make_async_copy(ref, ref, sem).wait()
 
     def wide_loaded(i):
-        all_of(wide.at[:, :, pl.ds(cuts[i] * tile, (cuts[i + 1] - cuts[i]) * tile)], load_sem.at[i])
+        all_of(wide.at[:, features(i), :], load_sem.at[i])
 
     for copy in own:
         copy.start()
@@ -82,7 +86,7 @@
     pl.when(has_left)(lambda: greet(left))
     with jax.named_scope("own"):
         all_of(every.at[pl.ds(0, R), :], own_sem.at[0])
-    for i in range(2):
+    for i in range(S):
         for copy in load_wide(i):
             copy.start()
     with jax.named_scope("barrier"):
@@ -94,11 +98,11 @@
         )
 
     def gather(b, j, way):
-        at = every.at[rows_of(b, j, c), :]
+        at = every.at[rows_of(b, c), features(j)]
         return remote(at, at, ag_send.at[way], ag_recv.at[b, j, c], (right, left, partner)[way])
 
     def gathered(b, j, q):
-        at = every.at[rows_of(b, j, q), :]
+        at = every.at[rows_of(b, q), features(j)]
         remote(at, at, ag_send.at[2], ag_recv.at[b, j, q], partner).wait_recv()
 
     @jax.named_scope("relay")
@@ -171,23 +175,24 @@
                 add_to_mine(b, d, d)
                 to_left(b, d).start()
 
-    def early(b, part):
+    def early_right(b, part):
         ahead = slice(0, 1) if part == 0 else slice(1, None)
         pl.when((p == 1) & has_right)(lambda: forward_right(b, range(C - 1, 0, -1)[ahead]))
+
+    def early_left(b, part):
+        ahead = slice(0, 1) if part == 0 else slice(1, None)
         pl.when((p == C - 2) & has_left)(lambda: forward_left(C - 1 - b, range(C - 1)[ahead]))
+
+    def early(b, part):
+        early_right(b, part)
+        early_left(b, part)
 
     def earlier():
         pl.when((p == 2) & has_right)(lambda: forward_right(1))
         pl.when((p == C - 3) & has_left)(lambda: forward_left(C - 2))
 
-    def pieces(b):
-        for j in range(S):
-            for q in range(2):
-                yield pl.ds((j * 2 + q) * Rs, Rs), rows_of(b, j, q), pl.ds(pl.multiple_of((2 * b + q) * R + j * Rs, Rs), Rs)
-
     def add_to_out(b, ref):
-        for at, _, to in pieces(b):
-            out[to, :] += ref[at, :].astype(f32)
+        acc[block_rows(b), :] += ref[...].astype(f32)
 
     @jax.named_scope("final")
     def final(b):
@@ -206,46 +211,78 @@
             landed_far()
             add_to_out(b, far)
 
+        out[block_rows(b), :] = acc[block_rows(b), :].astype(bf16)
+
     @jax.named_scope("norm")
-    def norm(b, j, q):
-        rows = every[rows_of(b, j, q), :].astype(f32)
-        scale = 1.0 / jnp.sqrt(jnp.mean(rows * rows, axis=1, keepdims=True) + 1e-05)
-        normed[rows_of(0, j, q), :] = (rows * gainv[...] * scale).astype(bf16)
-
-    def expand(s):
+    def prepare(b, j, q):
+        rows = every[rows_of(b, q), features(j)].astype(f32)
+        at = rows_of(0, q)
+        sums[j, at, :] = jnp.broadcast_to(jnp.sum(rows * rows, axis=1, keepdims=True), (R, 128))
+        normed[at, features(j)] = (rows * gainv[:, features(j)]).astype(bf16)
+
+    def expand(b, s, k):
+        def other_rows(j):
+            with jax.named_scope("await"):
+                gathered(b, j, 1 - c)
+
+        def products(x, j):
+            at = pl.ds(x * tile, tile)
+            return [jnp.dot(normed[:, features(j)], wide[y, features(j), at], preferred_element_type=f32) for y in range(2)]
+
+        pl.when(s == 0)(lambda: gain_copy.wait())
+        for j in range(S - 1):
+            prepare(b, j, c)
+            other_rows(j)
+            prepare(b, j, 1 - c)
+            if j == S - 2:
+                pl.when(inner & (s >= 1) & (k == s))(lambda: relay(s, S - 1))
+
+            @pl.when(s == 0)
+            def _():
+                with jax.named_scope("load"):
+                    wide_loaded(j)
+                    if j == 0:
+                        for d in range(C):
+                            load_down(d).start()
+
+            with jax.named_scope("expand0"):
+                for x in range(tiles):
+                    at = pl.ds(x * tile, tile)
+                    for y, product in enumerate(products(x, j)):
+                        partial[y, :, at] = product if j == 0 else partial[y, :, at] + product
+        pl.when(outer & (s >= 1))(lambda: relay(s, S - 1))
+        prepare(b, S - 1, c)
+        other_rows(S - 1)
+        prepare(b, S - 1, 1 - c)
+
+        @pl.when(s == 0)
+        def _():
+            with jax.named_scope("load"):
+                wide_loaded(S - 1)
+
         def part(i):
+            scale = 1.0 / jnp.sqrt(sum(sums[j] for j in range(S)) / D + 1e-05)
+            scale = jnp.concatenate([scale] * (tile // 128), axis=1)
             for x in range(cuts[i], cuts[i + 1]):
                 at = pl.ds(x * tile, tile)
-                gate = jnp.dot(normed[...], wide[0, :, at], preferred_element_type=f32)
-                up = jnp.dot(normed[...], wide[1, :, at], preferred_element_type=f32)
+                gate, up = [(partial[y, :, at] + product) * scale for y, product in enumerate(products(x, S - 1))]
                 hidden[s % 2, :, at] = (jax.nn.silu(gate) * up).astype(bf16)
 
-        @pl.when(s == 0)
-        def _():
-            with jax.named_scope("load"):
-                wide_loaded(0)
-                for d in range(C):
-                    load_down(d).start()
-
-        with jax.named_scope("expand0"):
+        with jax.named_scope("expand1"):
             part(0)
         share_hidden(s, 0).start()
-
-        @pl.when(s == 0)
-        def _():
-            with jax.named_scope("load"):
-                wide_loaded(1)
-
-        with jax.named_scope("expand1"):
+        pl.when(inner & (s >= 2) & (k != s))(lambda: relay(s, S - 1))
+        with jax.named_scope("expand2"):
             part(1)
         share_hidden(s, 1).start()
 
     def down(b, s):
+        turned = (p == 1) & (b == C - 1) if late else p < 0
         far_block = jnp.where(leans_left, (p == 0) & (b == C - 1), (p == C - 1) & (b == 0)) & (C > 2)
 
         def dest(i):
             i = jnp.where(far_block, 1 - i, i) if i < 2 else i
-            return jnp.where(leans_left, C - 1 - i, i)
+            return jnp.where(leans_left & jnp.logical_not(turned), C - 1 - i, i)
 
         def product(of, x, d):
             weight = dwv[x, :, pl.ds(pl.multiple_of(d * W, W), W)]
@@ -254,7 +291,7 @@
         @pl.when(s == 0)
         def _():
             with jax.named_scope("load"):
-                all_of(dwv.at[0], load_sem.at[2])
+                all_of(dwv.at[0], load_sem.at[S])
 
         with jax.named_scope("down0"):
             for d in range(C):
@@ -265,6 +302,8 @@
             with jax.named_scope("load"):
                 remote(dwv.at[1], dwv.at[1], down_send, down_recv, partner).wait_recv()
 
+        pl.when(outer & (s >= 1) & (s + 1 <= C - 1))(lambda: relay(s + 1, 0))
+        pl.when(s >= 2)(lambda: early_right(s - 1, 0))
         with jax.named_scope("peer"):
             for i in range(2):
                 share_hidden(s, i).wait_recv()
@@ -275,10 +314,11 @@
                     mine[b, d] = (half[d] + product(other, 1, d)).astype(bf16)
             for i in at:
                 first_send(b, dest(i))
+            if late and len(at) == 1:
+                pl.when(turned)(lambda: forward_left(C - 1))
         all_of(hidden.at[s % 2], pair_send)
 
-        for at, rows, to in pieces(b):
-            out[to, :] = every[rows, columns(me)].astype(f32) + mine[b, p, at, :].astype(f32)
+        acc[block_rows(b), :] = every[block_rows(b), columns(me)].astype(f32) + mine[b, p].astype(f32)
 
     for j in range(S):
         pl.when(has_right)(lambda: gather(p, j, 0).start())
@@ -293,33 +333,22 @@
         side = jnp.where((s <= 2 * both) & (s % 2 == 1), near, -near)
         b = p + side * k
 
-        def other(j):
+        def other_rows(j):
             with jax.named_scope("await"):
                 gathered(b, j, 1 - c)
 
-        for j in range(S - 1):
-            other(j)
-            if j == 0:
-                pl.when(s == 0)(lambda: gain_copy.wait())
-            for q in range(2):
-                norm(b, j, q)
-        pl.when(s >= 1)(lambda: relay(s, S - 1))
-        norm(b, S - 1, c)
-        other(S - 1)
-        norm(b, S - 1, 1 - c)
-        expand(s)
-        pl.when(s + 1 <= C - 1)(lambda: relay(s + 1, 0))
-        pl.when(s >= 2)(lambda: early(s - 1, 0))
+        expand(b, s, k)
+        pl.when((inner | (s == 0)) & (s + 1 <= C - 1))(lambda: relay(s + 1, 0))
+        pl.when(s >= 2)(lambda: early_left(s - 1, 0))
         pl.when(s == 3)(lambda: earlier())
         down(b, s)
         pl.when(s == 1)(lambda: early(0, 0))
         pl.when((s >= 1) & (s <= C - 2))(lambda: early(s - 1, 1))
 
-    late = C == 4
     for b in range(C):
         done = ((p == 1) & ((b <= C - 2) | late)) | ((p == 2) & (b == 1) & (C > 3))
         pl.when(inner & jnp.logical_not(done))(lambda: forward_right(b))
-        done = ((p == C - 2) & ((b <= C - 2) | late)) | ((p == C - 3) & (b == 1) & (C > 3))
+        done = ((p == C - 2) & ((b <= C - 2) | late)) | ((p == C - 3) & ((b == 1) & (C > 3) | (b == 0) & late))
         pl.when(inner & jnp.logical_not(done))(lambda: forward_left(C - 1 - b))
         if b == 0:
             early(C - 2, 1)
@@ -348,7 +377,7 @@
     dma = pltpu.SemaphoreType.DMA
     mixed = pl.pallas_call(
         functools.partial(block_kernel, n),
-        out_shape=pltpu.VMEM((n * R, W), f32),
+        out_shape=pltpu.VMEM((n * R, W), bf16),
         in_specs=[any_space] * 5,
         out_specs=vmem,
         scratch_shapes=[
@@ -357,13 +386,16 @@
             pltpu.VMEM((1, D), f32),
             pltpu.VMEM((C * T, D), bf16),
             pltpu.VMEM((T, D), bf16),
+            pltpu.VMEM((S, T, 128), f32),
+            pltpu.VMEM((2, T, F), f32),
             pltpu.VMEM((2, T, F), bf16),
             pltpu.VMEM((2, T, F), bf16),
             pltpu.VMEM((C, T, W), f32),
             pltpu.VMEM((C, C, T, W), bf16),
             pltpu.VMEM((C, C + 1, T, W), bf16),
             pltpu.VMEM((T, W), bf16),
-            dma((3,)),
+            pltpu.VMEM((C * T, W), f32),
+            dma((S + 1,)),
             dma((2,)),
             dma((C, S, 2)),
             dma((3,)),
@@ -377,7 +409,7 @@
         ],
         compiler_params=pltpu.CompilerParams(collective_id=0, has_side_effects=True, vmem_limit_bytes=VMEM_LIMIT),
     )(tokens, norm_gain[None, :], gate_weight, up_weight, down_weight)
-    return mixed.astype(bf16)
+    return mixed
 
 
 def solution(mesh):

time: 58 us -> 56.5 us (0.974)
  Pallas kernels: 57 us -> 55.5 us
  other arithmetic: 0.86 us -> 0 us
  local copies, waits for them, and re-layouts: 0 us -> 0.8 us
    pallas_call x1, Pallas kernels: 57 us -> 55.5 us  [on_device(): pl.pallas_call(functools.partial(block_kernel, n), out_shape=pltpu.VMEM((...]
    convert_element_type x1 -> x0, other arithmetic: 0.86 us -> none  [on_device(): return mixed.astype(bf16)]
    unnamed x0 -> x1, local copies, waits for them, and re-layouts: none -> 0.8 us
where the time goes in v5:
time: 56.5 us; the launch traced here: 56.3 us
  Pallas kernels  55.5 us (98%)
  local copies, waits for them, and re-layouts  0.8 us (1%)
    pallas_call x1, Pallas kernels, on_device(): pl.pallas_call(functools.partial(block_kernel, n), out_shape=pltpu.VMEM((...  55.5 us

profile of v5, /device:TPU:0, one launch (start us, length us, event | category | flops | bytes accessed | tf_op | source)
XLA Modules:
  0.0 56.3 jit_solution(5996700989548747906)
XLA Ops:
  0.0 55.5 %shard_map.55 = bf16[512,512]{1,0:T(8,128)(2,1)S(1)} custom-call(bf16[64,4096]{1,0:T(8,128)(2,1)} %tok.1, f32[1,4096]{1,0:T(1,128)} %bitcast.1, bf16[4096,1792]{1,0:T(8,128)(2,1)} %gw.1, bf16[4096,1792]{1,0:T(8,128)(2,1)} %uw.1, bf16[1792,4096]{1,0:T(8,128)(2,1)} %dw.1), custom_call_target="tpu_custom_call" | custom-call | tf_op jit(solution)/shard_map/pallas_call | solution.py:378
  55.5 0.8 %copy.7 = bf16[512,512]{1,0:T(8,128)(2,1)} copy(bf16[512,512]{1,0:T(8,128)(2,1)S(1)} %shard_map.55) | data formatting | bytes 1048576

commit v6 on v5

--- a/solution.py
+++ b/solution.py
@@ -33,7 +33,7 @@
     W = D // n
     tile = tile_of(F)
     tiles = F // tile
-    cuts = [0, (tiles + 1) // 2, tiles]
+    cuts = [0, tiles - tiles // 3, tiles]
     partner = (dp, 2 * p + (1 - c))
     right = (dp, lax.rem(me + 2, n))
     left = (dp, lax.rem(me + n - 2, n))
@@ -302,7 +302,7 @@
             with jax.named_scope("load"):
                 remote(dwv.at[1], dwv.at[1], down_send, down_recv, partner).wait_recv()
 
-        pl.when(outer & (s >= 1) & (s + 1 <= C - 1))(lambda: relay(s + 1, 0))
+        pl.when((s >= 1) & (s + 1 <= C - 1))(lambda: relay(s + 1, 0))
         pl.when(s >= 2)(lambda: early_right(s - 1, 0))
         with jax.named_scope("peer"):
             for i in range(2):
@@ -338,7 +338,7 @@
                 gathered(b, j, 1 - c)
 
         expand(b, s, k)
-        pl.when((inner | (s == 0)) & (s + 1 <= C - 1))(lambda: relay(s + 1, 0))
+        pl.when(s == 0)(lambda: relay(1, 0))
         pl.when(s >= 2)(lambda: early_left(s - 1, 0))
         pl.when(s == 3)(lambda: earlier())
         down(b, s)

time: 56.5 us -> 56.3 us (level)
  no operation moved by 1% of the time
where the time goes in v6:
time: 56.3 us; the launch traced here: 56.2 us
  Pallas kernels  55.4 us (98%)
  local copies, waits for them, and re-layouts  0.8 us (1%)
    pallas_call x1, Pallas kernels, on_device(): pl.pallas_call(functools.partial(block_kernel, n), out_shape=pltpu.VMEM((...  55.4 us

profile of v6, /device:TPU:0, one launch (start us, length us, event | category | flops | bytes accessed | tf_op | source)
XLA Modules:
  0.0 56.2 jit_solution(11390524253377998096)
XLA Ops:
  0.0 55.4 %shard_map.55 = bf16[512,512]{1,0:T(8,128)(2,1)S(1)} custom-call(bf16[64,4096]{1,0:T(8,128)(2,1)} %tok.1, f32[1,4096]{1,0:T(1,128)} %bitcast.1, bf16[4096,1792]{1,0:T(8,128)(2,1)} %gw.1, bf16[4096,1792]{1,0:T(8,128)(2,1)} %uw.1, bf16[1792,4096]{1,0:T(8,128)(2,1)} %dw.1), custom_call_target="tpu_custom_call" | custom-call | tf_op jit(solution)/shard_map/pallas_call | solution.py:378
  55.4 0.8 %copy.7 = bf16[512,512]{1,0:T(8,128)(2,1)} copy(bf16[512,512]{1,0:T(8,128)(2,1)S(1)} %shard_map.55) | data formatting | bytes 1048576

commit v7 on v6

--- a/solution.py
+++ b/solution.py
@@ -235,7 +235,7 @@
             other_rows(j)
             prepare(b, j, 1 - c)
             if j == S - 2:
-                pl.when(inner & (s >= 1) & (k == s))(lambda: relay(s, S - 1))
+                pl.when(s == 1)(lambda: relay(s, S - 1))
 
             @pl.when(s == 0)
             def _():
@@ -250,7 +250,7 @@
                     at = pl.ds(x * tile, tile)
                     for y, product in enumerate(products(x, j)):
                         partial[y, :, at] = product if j == 0 else partial[y, :, at] + product
-        pl.when(outer & (s >= 1))(lambda: relay(s, S - 1))
+        pl.when(outer & (s >= 2))(lambda: relay(s, S - 1))
         prepare(b, S - 1, c)
         other_rows(S - 1)
         prepare(b, S - 1, 1 - c)

time: 56.3 us -> 56.3 us (level)
  no operation moved by 1% of the time
where the time goes in v7:
time: 56.3 us; the launch traced here: 56.1 us
  Pallas kernels  55.3 us (98%)
  local copies, waits for them, and re-layouts  0.8 us (1%)
    pallas_call x1, Pallas kernels, on_device(): pl.pallas_call(functools.partial(block_kernel, n), out_shape=pltpu.VMEM((...  55.3 us

profile of v7, /device:TPU:0, one launch (start us, length us, event | category | flops | bytes accessed | tf_op | source)
XLA Modules:
  0.0 56.1 jit_solution(7335043000914241354)
XLA Ops:
  0.0 55.3 %shard_map.55 = bf16[512,512]{1,0:T(8,128)(2,1)S(1)} custom-call(bf16[64,4096]{1,0:T(8,128)(2,1)} %tok.1, f32[1,4096]{1,0:T(1,128)} %bitcast.1, bf16[4096,1792]{1,0:T(8,128)(2,1)} %gw.1, bf16[4096,1792]{1,0:T(8,128)(2,1)} %uw.1, bf16[1792,4096]{1,0:T(8,128)(2,1)} %dw.1), custom_call_target="tpu_custom_call" | custom-call | tf_op jit(solution)/shard_map/pallas_call | solution.py:378
  55.3 0.8 %copy.7 = bf16[512,512]{1,0:T(8,128)(2,1)} copy(bf16[512,512]{1,0:T(8,128)(2,1)S(1)} %shard_map.55) | data formatting | bytes 1048576
